TPU v7x, 128 devices: a whole 4x4x4 slice. The times are simulated.
128 devices in a mesh: row: 8 (over z_hi, x), col: 16 (over z_lo, y, core).
Axes of the slice: x: 4, y: 4, z: 4 (z_hi: 2, z_lo: 2; z = z_hi * 2 + z_lo), core: 2. Of those that a mesh axis runs over, the one named last changes fastest.
Arguments:
- features: bfloat16 [131072, 128], P(('row', 'col')), may hold values from -6 to 6
- pair_index: int32 [2, 16384], P(None, ('row', 'col')), may hold values from -1 to 127, as said below
- bins: int32 [16384, 128, 128], P(('row', 'col')), may hold values from 0 to 8, as said below
- plate_weight: bfloat16 [1024, 128], replicated, may hold values from -0.1875 to 0.1875
- tower_weight: bfloat16 [1024, 128], replicated, may hold values from -0.1875 to 0.1875
- norm_gain: float32 [128], replicated, may hold values from 0.1 to 1.9
- update_in: bfloat16 [256, 128], replicated, may hold values from -0.375 to 0.375
- update_out: bfloat16 [128, 128], replicated, may hold values from -0.5 to 0.5
Outputs:
- updated: bfloat16 [131072, 128], P(('row', 'col'))
Inputs may be any that keep to these rules, and one draw needn't show every extreme that they name: `pair_index`: row 0 is a cluster of the meeting device's plate (below 128), row 1 a cluster of its tower (below 64). The 128 slots of one meeting device hold its live pairs first and then -1 in both rows. No cluster pair is live twice on one device. Some device has all 128 slots live. `bins`: 8 marks an atom pair that is no neighbour.
All inputs are finite; a program needn't handle non-finite values.
Results may differ from a plain program's by a relative error of at most 0.008.
Values may be sent and summed in bfloat16 or wider, within the bound.
No kernel may reach another device: no remote copies, remote signals or barrier semaphores. Data moves between devices by JAX's collectives and lax.ppermute only.
A program may use at most 128 MiB of HBM per device.

v0:
```python
import jax
import jax.numpy as jnp
from jax import lax
from jax.experimental import pallas as pl
from jax.experimental.pallas import tpu as pltpu
from jax.sharding import PartitionSpec as P


D = 128
CLUSTER = 128
BINS = 8
SLOTS = 128
BLOCK = 8
HOME = 8
CUT = 5
MIB = 1024 * 1024


def live_count(index_ref):
    count = jnp.int32(0)
    for step in (128, 64, 32, 16, 8, 4, 2, 1):
        at = count + step
        inside = at <= SLOTS
        live = index_ref[0, jnp.minimum(at, SLOTS) - 1] >= 0
        count = jnp.where(inside & live, at, count)
    return count


def basis_of(level):
    one = jnp.ones((), jnp.bfloat16)
    zero = jnp.zeros((), jnp.bfloat16)
    level = level.astype(jnp.float32).astype(jnp.bfloat16)
    return [jnp.where(level == jnp.bfloat16(k), one, zero) for k in range(BINS)]


def plate_kernel(index_ref, bins_hbm, *refs):
    blocks_hbm, lines_hbm = refs[:8], refs[8:16]
    (weight_ref, mine_hbm, theirs_hbm, line_hbm, bins_ref, tower_ref, far_ref, acc_ref, out_ref,
     line_ref, sems, tower_sems, out_sems, line_sems) = refs[16:]
    row, col = index_ref[0, SLOTS], index_ref[1, SLOTS]
    row_z, row_x = row // 4, row % 4
    col_z, col_y, core = col // 8, (col // 2) % 4, col % 2

    def block_copy(j):
        source = ((row_z + 2 - j // 4) % 2) * 4 + (row_x + 4 - j % 4) % 4
        rows = pl.ds(pl.multiple_of(source * 1024, 1024), 1024)
        return pltpu.make_async_copy(blocks_hbm[j], tower_ref.at[rows], tower_sems.at[j])

    def line_copy(j):
        return pltpu.make_async_copy(lines_hbm[j], line_ref.at[pl.ds(j * 1024, 1024)], line_sems.at[j])

    line_out = pltpu.make_async_copy(line_ref, line_hbm, line_sems.at[8])

    for j in range(8):
        block_copy(j).start()
    for j in range(8):
        line_copy(j).start()
    count = live_count(index_ref)
    blocks = (count + BLOCK - 1) // BLOCK

    def bins_copy(block):
        part = pl.ds(block * BLOCK, BLOCK)
        return pltpu.make_async_copy(bins_hbm.at[part], bins_ref.at[part], sems.at[block])

    def start(block, _):
        bins_copy(block).start()
        return 0

    lax.fori_loop(0, blocks, start, 0)
    acc_ref[SLOTS] = jnp.zeros((CLUSTER, D), jnp.float32)

    def project(source, _):
        j = ((row_z + 2 - source // 4) % 2) * 4 + (row_x + 4 - source % 4) % 4
        at = pl.multiple_of(source * 1024, 1024)
        pltpu.make_async_copy(blocks_hbm[0], tower_ref.at[pl.ds(at, 1024)], tower_sems.at[j]).wait()
        for u in range(16):
            acc_ref[source * 16 + u] = jnp.zeros((CLUSTER, D), jnp.float32)
        for half in range(2):
            rows = tower_ref[pl.ds(at + half * 512, 512), :]
            for k in range(0, BINS, 2):
                both = jnp.dot(
                    rows, weight_ref[:, k * D : (k + 2) * D], preferred_element_type=jnp.float32
                ).astype(jnp.bfloat16)
                for u in range(4):
                    part = both[u * CLUSTER : (u + 1) * CLUSTER]
                    to = source * 8 + half * 4 + u
                    far_ref[to, k * CLUSTER : (k + 1) * CLUSTER, :] = part[:, :D]
                    far_ref[to, (k + 1) * CLUSTER : (k + 2) * CLUSTER, :] = part[:, D:]
        return 0

    lax.fori_loop(0, 8, project, 0)
    for j in range(8):
        line_copy(j).wait()
    line_out.start()

    def block_step(block, _):
        bins_copy(block).wait()
        for u in range(BLOCK):
            slot = block * BLOCK + u
            plate_at = index_ref[0, slot]
            plate_at = jnp.where(plate_at < 0, SLOTS, plate_at)
            tower_at = jnp.maximum(index_ref[1, slot], 0)
            basis = jnp.concatenate(basis_of(bins_ref[slot]), axis=1)
            message = jnp.dot(basis, far_ref[tower_at], preferred_element_type=jnp.float32)
            acc_ref[plate_at] += message
        return 0

    lax.fori_loop(0, blocks, block_step, 0)

    def out_copy(n):
        j = n % 8
        dest = (theirs_hbm, mine_hbm)[n // 8]
        return pltpu.make_async_copy(
            out_ref.at[pl.ds(n * 1024, 1024)], dest.at[pl.ds(j * 1024, 1024)], out_sems.at[n]
        )

    for n in range(16):
        j = n % 8
        side = 1 - core if n < 8 else core
        home = ((col_z + j % 2) % 2) * 8 + ((col_y + j // 2) % 4) * 2 + side
        for u in range(8):
            at = (n * 8 + u) * CLUSTER
            out_ref[at : at + CLUSTER, :] = acc_ref[home * 8 + u].astype(jnp.bfloat16)
        out_copy(n).start()
    for n in range(16):
        out_copy(n).wait()
    line_out.wait()


def tower_kernel(part, index_ref, bins_hbm, mine_hbm, theirs_hbm, weight_ref, *refs):
    out_refs = refs[: 1 if part == 0 else 4]
    bins_ref, plate_ref, acc_ref, near_a, near_b, slot_ref, from_ref, to_ref, sems, plate_sems = refs[len(out_refs) :]
    col = index_ref[1, SLOTS]
    col_z, col_y, core = col // 8, (col // 2) % 4, col % 2

    def block_copy(n):
        j = n % 8
        side = core if n < 8 else 1 - core
        source = ((col_z + 2 - j % 2) % 2) * 8 + ((col_y + 4 - j // 2) % 4) * 2 + side
        rows = pl.ds(pl.multiple_of(source * 1024, 1024), 1024)
        block = (mine_hbm, theirs_hbm)[n // 8].at[pl.ds(j * 1024, 1024)]
        return pltpu.make_async_copy(block, plate_ref.at[rows], plate_sems.at[n])

    for n in range(16):
        block_copy(n).start()
    live = live_count(index_ref)
    spare = acc_ref.shape[0] - 1

    first = CUT * part
    width = CUT if part == 0 else HOME - CUT
    for u in range(BLOCK):
        to_ref[u] = spare

    def pick(i, found):
        for u in range(BLOCK):
            slot = i * BLOCK + u
            tower_at = index_ref[1, slot]
            inner = tower_at % HOME
            slot_ref[found] = slot
            from_ref[found] = index_ref[0, slot]
            to_ref[found + BLOCK] = (tower_at // HOME) * width + inner - first
            mine = (tower_at >= 0) & (inner >= first) & (inner < first + width)
            found = found + jnp.where(mine, 1, 0)
        return found

    count = lax.fori_loop(0, (live + BLOCK - 1) // BLOCK, pick, jnp.int32(0))
    for u in range(BLOCK):
        slot_ref[count + u] = 0
        from_ref[count + u] = 0
        to_ref[count + u + BLOCK] = spare
    blocks = (count + BLOCK - 1) // BLOCK

    def start(block, _):
        for u in range(BLOCK):
            at = block * BLOCK + u
            pltpu.make_async_copy(bins_hbm.at[slot_ref[at]], bins_ref.at[at], sems.at[block]).start()
        return 0

    lax.fori_loop(0, blocks, start, 0)

    def zero(i, _):
        for u in range(8):
            acc_ref[i * 8 + u] = jnp.zeros((D, CLUSTER), jnp.float32)
        return 0

    lax.fori_loop(0, spare // 8, zero, 0)
    acc_ref[spare] = jnp.zeros((D, CLUSTER), jnp.float32)
    near_b[...] = jnp.zeros(near_b.shape, jnp.bfloat16)
    for n in range(16):
        block_copy(n).wait()

    def gather_near(base, near_ref):
        for u in range(BLOCK // 2):
            at = base + u
            rows = plate_ref[pl.ds(pl.multiple_of(from_ref[at] * CLUSTER, CLUSTER), CLUSTER), :]
            flipped = rows.T
            basis = basis_of(bins_ref[at])
            for k in range(0, BINS, 2):
                near = jnp.dot(
                    flipped, jnp.concatenate(basis[k : k + 2], axis=1), preferred_element_type=jnp.float32
                ).astype(jnp.bfloat16)
                for h in range(2):
                    near_ref[
                        u // 2, (k + h) * D : (k + h + 1) * D, (u % 2) * CLUSTER : (u % 2 + 1) * CLUSTER
                    ] = near[:, h * CLUSTER : (h + 1) * CLUSTER]

    def send_on(base, near_ref):
        for pair in range(BLOCK // 4):
            message = jnp.dot(weight_ref[...], near_ref[pair], preferred_element_type=jnp.float32)
            for u in range(2):
                acc_ref[to_ref[base + pair * 2 + u + BLOCK]] += message[:, u * CLUSTER : (u + 1) * CLUSTER]

    def block_step(block, _):
        base = block * BLOCK
        pltpu.make_async_copy(
            bins_hbm.at[pl.ds(0, BLOCK)], bins_ref.at[pl.ds(base, BLOCK)], sems.at[block]
        ).wait()
        gather_near(base, near_a)
        send_on(base - BLOCK // 2, near_b)
        gather_near(base + BLOCK // 2, near_b)
        send_on(base, near_a)
        return 0

    lax.fori_loop(0, blocks, block_step, 0)
    send_on(blocks * BLOCK - BLOCK // 2, near_b)

    row = index_ref[0, SLOTS]
    for j in range(8):
        home = j if part == 0 else ((row // 4 + j // 4) % 2) * 4 + (row % 4 + j % 4) % 4
        out_ref = out_refs[0 if part == 0 else j % 4]
        for u in range(width):
            at = ((j if part == 0 else j // 4) * width + u) * CLUSTER
            out_ref[at : at + CLUSTER, :] = acc_ref[home * width + u].astype(jnp.bfloat16)


def add_kernel(mine_hbm, theirs_hbm, *refs):
    outs, (mine_ref, theirs_ref, sum_ref, in_sems, out_sems) = refs[:4], refs[4:]
    ins = []
    for j in range(4):
        rows = pl.ds(j * 2048, 2048)
        ins.append(
            (
                pltpu.make_async_copy(mine_hbm.at[rows], mine_ref.at[rows], in_sems.at[0, j]),
                pltpu.make_async_copy(theirs_hbm.at[rows], theirs_ref.at[rows], in_sems.at[1, j]),
            )
        )
    order = (1, 3, 2, 0)
    for j in order:
        for copy in ins[j]:
            copy.start()
    back = []
    for j in order:
        for copy in ins[j]:
            copy.wait()
        rows = pl.ds(j * 2048, 2048)
        total = mine_ref[rows, :].astype(jnp.float32) + theirs_ref[rows, :].astype(jnp.float32)
        sum_ref[rows, :] = total.astype(jnp.bfloat16)
        back.append(pltpu.make_async_copy(sum_ref.at[rows], outs[j], out_sems.at[j]))
        back[-1].start()
    for copy in back:
        copy.wait()


def updated_rows(flipped, rows, side_refs, features_ref, gain_ref, in_ref, last_ref):
    incoming = flipped.T
    for ref in side_refs:
        incoming += ref[rows, :].astype(jnp.float32)
    scale = lax.rsqrt(jnp.mean(incoming * incoming, axis=1, keepdims=True) + 1e-06)
    normed = (incoming * scale * gain_ref[...]).astype(jnp.bfloat16)
    features = features_ref[rows, :]
    mixed = jnp.dot(
        jnp.concatenate([features, normed], axis=1), in_ref[...], preferred_element_type=jnp.float32
    )
    hidden = (mixed / (1.0 + jnp.exp(-mixed))).astype(jnp.bfloat16)
    change = jnp.dot(hidden, last_ref[...], preferred_element_type=jnp.float32)
    return (features.astype(jnp.float32) + change).astype(jnp.bfloat16)


def early_kernel(arrived_ref, *refs):
    side_refs, (features_ref, gain_ref, in_ref, last_ref, out_hbm, out_ref, sem) = refs[:5], refs[5:]
    for c in range(CUT):
        rows = slice(c * CLUSTER, (c + 1) * CLUSTER)
        flipped = arrived_ref[0, rows, :].astype(jnp.float32)
        for r in range(1, 8):
            flipped += arrived_ref[r, rows, :].astype(jnp.float32)
        out_ref[rows, :] = updated_rows(flipped, rows, side_refs, features_ref, gain_ref, in_ref, last_ref)
    copy = pltpu.make_async_copy(out_ref, out_hbm.at[pl.ds(0, CUT * CLUSTER)], sem)
    copy.start()
    copy.wait()


def late_kernel(early_hbm, *refs):
    arrived_refs, side_refs, refs = refs[:5], refs[5:10], refs[10:]
    features_ref, gain_ref, in_ref, last_ref, out_hbm, out_ref, sem = refs
    for c in range(HOME - CUT):
        at = slice(c * CLUSTER, (c + 1) * CLUSTER)
        rows = slice((CUT + c) * CLUSTER, (CUT + c + 1) * CLUSTER)
        flipped = arrived_refs[0][at, :].astype(jnp.float32)
        for r in range(1, 5):
            flipped += arrived_refs[r][at, :].astype(jnp.float32)
        out_ref[at, :] = updated_rows(flipped, rows, side_refs, features_ref, gain_ref, in_ref, last_ref)
    copy = pltpu.make_async_copy(out_ref, out_hbm.at[pl.ds(CUT * CLUSTER, (HOME - CUT) * CLUSTER)], sem)
    copy.start()
    copy.wait()


SMEM = pl.BlockSpec(memory_space=pltpu.SMEM)
VMEM = pl.BlockSpec(memory_space=pltpu.VMEM)
HBM = pl.BlockSpec(memory_space=pltpu.HBM)
PARAMS = pltpu.CompilerParams(vmem_limit_bytes=50 * MIB)


def cost(flops, data):
    return pl.CostEstimate(flops=flops, bytes_accessed=data, transcendentals=0)


def plate_messages(pair_index, bins, blocks, lines, weight):
    half = jax.ShapeDtypeStruct((8192, D), jnp.bfloat16)
    return pl.pallas_call(
        plate_kernel,
        out_shape=(half, half, half),
        in_specs=[SMEM, HBM, *[HBM] * 16, VMEM],
        out_specs=(HBM, HBM, HBM),
        scratch_shapes=[
            pltpu.VMEM((SLOTS, CLUSTER, CLUSTER), jnp.int32),
            pltpu.VMEM((8192, D), jnp.bfloat16),
            pltpu.VMEM((64, BINS * CLUSTER, D), jnp.bfloat16),
            pltpu.VMEM((SLOTS + 1, CLUSTER, D), jnp.float32),
            pltpu.VMEM((16384, D), jnp.bfloat16),
            pltpu.VMEM((8192, D), jnp.bfloat16),
            pltpu.SemaphoreType.DMA((SLOTS // BLOCK,)),
            pltpu.SemaphoreType.DMA((8,)),
            pltpu.SemaphoreType.DMA((16,)),
            pltpu.SemaphoreType.DMA((9,)),
        ],
        compiler_params=PARAMS,
        cost_estimate=cost(25_000_000_000, 15_000_000),
        name="plate_messages",
    )(pair_index, bins, *blocks, *lines, weight)


def tower_messages(part, pair_index, bins, mine, theirs, weight):
    clusters = 8 * (CUT if part == 0 else HOME - CUT)
    outs = 1 if part == 0 else 4
    near = pltpu.VMEM((BLOCK // 4, BINS * D, 2 * CLUSTER), jnp.bfloat16)
    return pl.pallas_call(
        lambda *refs: tower_kernel(part, *refs),
        out_shape=[jax.ShapeDtypeStruct((clusters * CLUSTER // outs, D), jnp.bfloat16)] * outs,
        in_specs=[SMEM, HBM, HBM, HBM, VMEM],
        out_specs=[VMEM] * outs,
        scratch_shapes=[
            pltpu.VMEM((SLOTS, CLUSTER, CLUSTER), jnp.int32),
            pltpu.VMEM((16384, D), jnp.bfloat16),
            pltpu.VMEM((clusters + 1, D, CLUSTER), jnp.float32),
            near,
            near,
            pltpu.SMEM((SLOTS + BLOCK,), jnp.int32),
            pltpu.SMEM((SLOTS + BLOCK,), jnp.int32),
            pltpu.SMEM((SLOTS + 2 * BLOCK,), jnp.int32),
            pltpu.SemaphoreType.DMA((SLOTS // BLOCK,)),
            pltpu.SemaphoreType.DMA((16,)),
        ],
        compiler_params=pltpu.CompilerParams(vmem_limit_bytes=60 * MIB),
        cost_estimate=cost(15_000_000_000, 10_000_000),
    )(pair_index, bins, mine, theirs, weight)


def core_sum(mine, theirs):
    return pl.pallas_call(
        add_kernel,
        out_shape=tuple(jax.ShapeDtypeStruct((2048, D), jnp.bfloat16) for _ in range(4)),
        in_specs=[HBM, HBM],
        out_specs=tuple(HBM for _ in range(4)),
        scratch_shapes=[
            pltpu.VMEM((8192, D), jnp.bfloat16),
            pltpu.VMEM((8192, D), jnp.bfloat16),
            pltpu.VMEM((8192, D), jnp.bfloat16),
            pltpu.SemaphoreType.DMA((2, 4)),
            pltpu.SemaphoreType.DMA((4,)),
        ],
        compiler_params=PARAMS,
        cost_estimate=cost(2_000_000_000, 6_000_000),
        name="core_sum",
    )(mine, theirs)


def update(part, arrived, own_rows, across, features, gain, update_in, update_out):
    rows = (CUT if part == 0 else HOME - CUT) * CLUSTER
    return pl.pallas_call(
        early_kernel if part == 0 else late_kernel,
        out_shape=jax.ShapeDtypeStruct((1024, D), jnp.bfloat16),
        grid=(1,),
        in_specs=([HBM] + [pl.BlockSpec((rows, D), lambda i: (0, 0))] * 5 if part else [VMEM])
        + [pl.BlockSpec((1024, D), lambda i: (0, 0))] * 4
        + [VMEM] * 5,
        out_specs=HBM,
        scratch_shapes=[pltpu.VMEM((rows, D), jnp.bfloat16), pltpu.SemaphoreType.DMA(())],
        input_output_aliases={0: 0} if part else {},
        compiler_params=pltpu.CompilerParams(vmem_limit_bytes=12 * MIB),
        cost_estimate=cost(2_000_000_000, 4_000_000),
    )(*arrived, *own_rows, across, features, gain, update_in, update_out)


def along_col(value, dz, dy):
    pairs = [
        (z * 8 + y * 2 + c, ((z + dz) % 2) * 8 + ((y + dy) % 4) * 2 + c)
        for z in range(2)
        for y in range(4)
        for c in range(2)
    ]
    return lax.ppermute(value, "col", pairs)


def along_row(value, dz, dx):
    pairs = [(z * 4 + x, ((z + dz) % 2) * 4 + (x + dx) % 4) for z in range(2) for x in range(4)]
    return lax.ppermute(value, "row", pairs)


def to_other_core(value):
    return lax.ppermute(value, "col", [(i, i ^ 1) for i in range(16)])


def over_rows(part):
    return lax.all_to_all(
        part.reshape(8, -1, D), "row", split_axis=0, concat_axis=0, tiled=True
    )


def layer(
    features, pair_index, bins, plate_weight, tower_weight, norm_gain, update_in, update_out
):
    place = jnp.stack([lax.axis_index("row"), lax.axis_index("col")]).astype(jnp.int32)
    table = jnp.concatenate([pair_index, jnp.broadcast_to(place[:, None], (2, SLOTS))], axis=1)
    plate_cat = plate_weight.reshape(BINS, D, D).transpose(1, 0, 2).reshape(D, BINS * D)
    tower_flip = tower_weight.T
    row_far = along_row(features, 1, 0)
    col_far = along_col(features, 1, 0)
    row_near = [along_row(features, 0, d) for d in (1, 3)]
    col_near = [along_col(features, 0, d) for d in (1, 3)]
    row_more = [along_row(row_far, 0, d) for d in (1, 3)]
    col_more = [along_col(col_far, 0, d) for d in (1, 3)]
    row_near.append(along_row(row_near[0], 0, 1))
    col_near.append(along_col(col_near[0], 0, 1))
    row_more.append(along_row(row_far, 0, 2))
    col_more.append(along_col(col_far, 0, 2))
    tower_blocks = [features, row_near[0], row_near[2], row_near[1], row_far, row_more[0], row_more[2], row_more[1]]
    lines = [features, col_far, col_near[0], col_more[0], col_near[2], col_more[2], col_near[1], col_more[1]]
    part_mine, part_theirs, plate_mine = plate_messages(
        table, bins, tower_blocks, lines, plate_cat
    )
    part_back = to_other_core(part_theirs)
    plate_theirs = to_other_core(plate_mine)
    first = tower_messages(0, table, bins, plate_mine, plate_theirs, tower_flip)
    own, *sums = core_sum(part_mine, part_back)
    back = [along_col(sums[d - 1], 0, d) for d in (1, 3, 2)]
    second = tower_messages(1, table, bins, plate_mine, plate_theirs, tower_flip)
    first_back = over_rows(first[0])
    second_back = [along_row(second[d], 0, d) for d in (1, 3, 2)]
    half = (HOME - CUT) * CLUSTER
    second_far = second[0][half:].astype(jnp.float32)
    for part in second_back:
        second_far = second_far + part[half:].astype(jnp.float32)
    second_far = second_far.astype(jnp.bfloat16)
    second_far = along_row(second_far, 1, 0)
    far = own[1024:].astype(jnp.float32)
    for part in back:
        far = far + part[1024:].astype(jnp.float32)
    far = far.astype(jnp.bfloat16)
    across = along_col(far, 1, 0)
    rest = ([own, *back], across, features, norm_gain.reshape(1, D), update_in, update_out)
    early = update(0, [first_back], *rest)
    return update(1, [early, second[0], *second_back, second_far], *rest)


def solution(mesh):
    placed = (
        P(("row", "col"), None),
        P(None, ("row", "col")),
        P(("row", "col"), None, None),
        P(),
        P(),
        P(),
        P(),
        P(),
    )
    return jax.shard_map(layer, mesh=mesh, in_specs=placed, out_specs=P(("row", "col"), None), check_vma=False)
```

profile of v0, /device:TPU:8, one launch (start us, length us, event | category | flops | bytes accessed | tf_op | source)
XLA Modules:
  0.0 135.1 jit_solution(11518114623321866582)
XLA Ops:
  0.3 1.7 %collective-permute-start.8 = (bf16[1024,128]{1,0:T(8,128)(2,1)}, bf16[1024,128]{1,0:T(8,128)(2,1)S(1)}, u32[]{:S(2)}, u32[]{:S(2)}) collective-permute-start(bf16[1024,128]{1,0:T(8,128)(2,1)} %refs_10_.1), channel_id=1, source_target_pairs={{0,2},{1,3},{2,4},{3,5},{4,6},{5,7},{6,0},{7,1},{8,10},{9,11},{10,... | collective-permute-start | bytes 786440 | tf_op jit(solution)/shard_map/ppermute | solution.py:411
  2.0 1.9 %collective-permute-start.7 = (bf16[1024,128]{1,0:T(8,128)(2,1)}, bf16[1024,128]{1,0:T(8,128)(2,1)S(1)}, u32[]{:S(2)}, u32[]{:S(2)}) collective-permute-start(bf16[1024,128]{1,0:T(8,128)(2,1)} %refs_10_.1), channel_id=1, source_target_pairs={{0,8},{1,9},{2,10},{3,11},{4,12},{5,13},{6,14},{7,15},{8,0},{9,1},... | collective-permute-start | bytes 786440 | tf_op jit(solution)/shard_map/ppermute | solution.py:411
  3.9 3.6 %collective-permute-start.3 = (bf16[1024,128]{1,0:T(8,128)(2,1)}, bf16[1024,128]{1,0:T(8,128)(2,1)S(1)}, u32[]{:S(2)}, u32[]{:S(2)}) collective-permute-start(bf16[1024,128]{1,0:T(8,128)(2,1)} %refs_10_.1), channel_id=1, source_target_pairs={{0,64},{16,80},{32,96},{48,112},{64,0},{80,16},{96,32},{112,48},{1... | collective-permute-start | bytes 786440 | tf_op jit(solution)/shard_map/ppermute | solution.py:416
  7.5 2.8 %collective-permute-start.2 = (bf16[1024,128]{1,0:T(8,128)(2,1)}, bf16[1024,128]{1,0:T(8,128)(2,1)S(1)}, u32[]{:S(2)}, u32[]{:S(2)}) collective-permute-start(bf16[1024,128]{1,0:T(8,128)(2,1)} %refs_10_.1), channel_id=1, source_target_pairs={{0,48},{16,0},{32,16},{48,32},{64,112},{80,64},{96,80},{112,96},{1... | collective-permute-start | bytes 786440 | tf_op jit(solution)/shard_map/ppermute | solution.py:416
  12.9 6.0 %collective-permute-done.3.refs_4_ = bf16[1024,128]{1,0:T(8,128)(2,1)S(1)} collective-permute-done((bf16[1024,128]{1,0:T(8,128)(2,1)}, bf16[1024,128]{1,0:T(8,128)(2,1)S(1)}, u32[]{:S(2)}, u32[]{:S(2)}) %collective-permute-start.3) | collective-permute-done | bytes 262176 | tf_op jit(solution)/shard_map/ppermute | solution.py:416
  18.8 3.5 %collective-permute-start.11 = (bf16[1024,128]{1,0:T(8,128)(2,1)S(1)}, bf16[1024,128]{1,0:T(8,128)(2,1)S(1)}, u32[]{:S(2)}, u32[]{:S(2)}) collective-permute-start(bf16[1024,128]{1,0:T(8,128)(2,1)S(1)} %collective-permute-done.7.refs_9_), channel_id=1, source_target_pairs={{0,4},{1,5},{2,6},{3,7},{4,0},{5,1},{6,2},{7,3},{8,12},{9,13},{10,... | collective-permute-start | bytes 786440 | tf_op jit(solution)/shard_map/ppermute | solution.py:411
  22.3 2.8 %collective-permute-start.6 = (bf16[1024,128]{1,0:T(8,128)(2,1)S(1)}, bf16[1024,128]{1,0:T(8,128)(2,1)S(1)}, u32[]{:S(2)}, u32[]{:S(2)}) collective-permute-start(bf16[1024,128]{1,0:T(8,128)(2,1)S(1)} %collective-permute-done.3.refs_4_), channel_id=1, source_target_pairs={{0,48},{16,0},{32,16},{48,32},{64,112},{80,64},{96,80},{112,96},{1... | collective-permute-start | bytes 786440 | tf_op jit(solution)/shard_map/ppermute | solution.py:416
  32.7 1.9 %collective-permute-done.6.refs_7_ = bf16[1024,128]{1,0:T(8,128)(2,1)S(1)} collective-permute-done((bf16[1024,128]{1,0:T(8,128)(2,1)S(1)}, bf16[1024,128]{1,0:T(8,128)(2,1)S(1)}, u32[]{:S(2)}, u32[]{:S(2)}) %collective-permute-start.6) | collective-permute-done | bytes 262176 | tf_op jit(solution)/shard_map/ppermute | solution.py:416
  35.9 3.1 %collective-permute-done.4.refs_5_ = bf16[1024,128]{1,0:T(8,128)(2,1)S(1)} collective-permute-done((bf16[1024,128]{1,0:T(8,128)(2,1)S(1)}, bf16[1024,128]{1,0:T(8,128)(2,1)S(1)}, u32[]{:S(2)}, u32[]{:S(2)}) %collective-permute-start.4) | collective-permute-done | bytes 262176 | tf_op jit(solution)/shard_map/ppermute | solution.py:416
  38.9 5.2 %collective-permute-done.1.refs_2_ = bf16[1024,128]{1,0:T(8,128)(2,1)} collective-permute-done((bf16[1024,128]{1,0:T(8,128)(2,1)S(1)}, bf16[1024,128]{1,0:T(8,128)(2,1)}, u32[]{:S(2)}, u32[]{:S(2)}) %collective-permute-start.1) | collective-permute-done | bytes 262176 | tf_op jit(solution)/shard_map/ppermute | solution.py:416
  45.0 21.4 %plate_messages.1 = (bf16[8192,128]{1,0:T(8,128)(2,1)}, bf16[8192,128]{1,0:T(8,128)(2,1)}, bf16[8192,128]{1,0:T(8,128)(2,1)}) custom-call(s32[2,256]{1,0:T(2,128)S(1)} %pad_add_fusion.index_ref.refs_0_, s32[128,128,128]{2,1,0:T(8,128)} %refs_1_.3, bf16[1024,128]{1,0:T(8,128)(2,1)S(1)} %copy-done.8, bf16[1024,128]{1,0:T(8,128)(2,1)S(1)} %collective-permute-done.refs_1_, ...), custom_call_target="tpu_custom_call" | custom-call | flops 24999999488 | bytes 15000000 | tf_op jit(solution)/shard_map/plate_messages/pallas_call | solution.py:319
  67.0 1.8 %copy.11 = bf16[1024,128]{0,1:T(8,128)(2,1)} copy(bf16[1024,128]{1,0:T(8,128)(2,1)} %param.12) | data formatting | bytes 524288 | tf_op args[4]
  68.8 2.1 %collective-permute-done.15.theirs_hbm = bf16[8192,128]{1,0:T(8,128)(2,1)S(1)} collective-permute-done((bf16[8192,128]{1,0:T(8,128)(2,1)}, bf16[8192,128]{1,0:T(8,128)(2,1)S(1)}, u32[]{:S(2)}, u32[]{:S(2)}) %collective-permute-start.15) | collective-permute-done | bytes 2097184 | tf_op jit(solution)/shard_map/ppermute | solution.py:420
  72.3 2.9 %core_sum.1 = (bf16[2048,128]{1,0:T(8,128)(2,1)S(1)}, bf16[2048,128]{1,0:T(8,128)(2,1)}, bf16[2048,128]{1,0:T(8,128)(2,1)}, bf16[2048,128]{1,0:T(8,128)(2,1)}) custom-call(bf16[8192,128]{1,0:T(8,128)(2,1)} %get-tuple-element.17.mine_hbm, bf16[8192,128]{1,0:T(8,128)(2,1)} %copy-done.16), custom_call_target="tpu_custom_call" | custom-call | flops 2000000000 | bytes 6000000 | tf_op jit(solution)/shard_map/core_sum/pallas_call | solution.py:369
  75.2 2.0 %collective-permute-start.17 = (bf16[2048,128]{1,0:T(8,128)(2,1)}, bf16[2048,128]{1,0:T(8,128)(2,1)S(1)}, u32[]{:S(2)}, u32[]{:S(2)}) collective-permute-start(bf16[2048,128]{1,0:T(8,128)(2,1)} %get-tuple-element.21), channel_id=1, source_target_pairs={{0,6},{1,7},{2,0},{3,1},{4,2},{5,3},{6,4},{7,5},{8,14},{9,15},{10,... | collective-permute-start | bytes 1572872 | tf_op jit(solution)/shard_map/ppermute | solution.py:411
  77.2 1.9 %collective-permute-start.18 = (bf16[2048,128]{1,0:T(8,128)(2,1)}, bf16[2048,128]{1,0:T(8,128)(2,1)S(1)}, u32[]{:S(2)}, u32[]{:S(2)}) collective-permute-start(bf16[2048,128]{1,0:T(8,128)(2,1)} %get-tuple-element.22), channel_id=1, source_target_pairs={{0,4},{1,5},{2,6},{3,7},{4,0},{5,1},{6,2},{7,3},{8,12},{9,13},{10,... | collective-permute-start | bytes 1572872 | tf_op jit(solution)/shard_map/ppermute | solution.py:411
  79.1 16.0 %shard_map.82 = bf16[5120,128]{1,0:T(8,128)(2,1)} custom-call(s32[2,256]{1,0:T(2,128)} %copy-done.7, s32[128,128,128]{2,1,0:T(8,128)} %refs_1_.3, bf16[8192,128]{1,0:T(8,128)(2,1)} %get-tuple-element.16.refs_2_, bf16[8192,128]{1,0:T(8,128)(2,1)} %collective-permute-done.14.refs_3_, bf16[128,1024]{1,0:T(8,128)(2,1)} %bitcast.17), custom_call_target="tpu_custom_call" | custom-call | flops 15000000512 | bytes 10000000 | tf_op jit(solution)/shard_map/pallas_call | solution.py:346
  95.1 3.8 %all-to-all-start = ((bf16[8,640,128]{2,1,0:T(8,128)(2,1)}), bf16[8,640,128]{2,1,0:T(8,128)(2,1)S(1)}, u32[]{:S(2)}, u32[]{:S(2)}) async-start(bf16[8,640,128]{2,1,0:T(8,128)(2,1)} %bitcast.13), calls=%async_computation | async-start | bytes 2621440 | tf_op jit(solution)/shard_map/all_to_all | solution.py:424
  98.9 12.5 %shard_map.84 = (bf16[768,128]{1,0:T(8,128)(2,1)}, bf16[768,128]{1,0:T(8,128)(2,1)}, bf16[768,128]{1,0:T(8,128)(2,1)}, bf16[768,128]{1,0:T(8,128)(2,1)}) custom-call(s32[2,256]{1,0:T(2,128)} %copy-done.7, s32[128,128,128]{2,1,0:T(8,128)} %refs_1_.3, bf16[8192,128]{1,0:T(8,128)(2,1)} %get-tuple-element.16.refs_2_, ...), custom_call_target="tpu_custom_call" | custom-call | flops 15000000512 | bytes 10000000 | tf_op jit(solution)/shard_map/pallas_call | solution.py:346
  111.5 3.2 %collective-permute-start.21 = (bf16[768,128]{1,0:T(8,128)(2,1)}, bf16[768,128]{1,0:T(8,128)(2,1)S(1)}, u32[]{:S(2)}, u32[]{:S(2)}) collective-permute-start(bf16[768,128]{1,0:T(8,128)(2,1)} %get-tuple-element.25), channel_id=1, source_target_pairs={{0,48},{16,0},{32,16},{48,32},{64,112},{80,64},{96,80},{112,96},{1... | collective-permute-start | bytes 589832 | tf_op jit(solution)/shard_map/ppermute | solution.py:416
  115.1 5.2 %collective-permute-done.20.refs_1_ = bf16[768,128]{1,0:T(8,128)(2,1)S(1)} collective-permute-done((bf16[768,128]{1,0:T(8,128)(2,1)}, bf16[768,128]{1,0:T(8,128)(2,1)S(1)}, u32[]{:S(2)}, u32[]{:S(2)}) %collective-permute-start.20) | collective-permute-done | bytes 196640 | tf_op jit(solution)/shard_map/ppermute | solution.py:416
  120.3 1.9 %collective-permute-done.21.refs_2_ = bf16[768,128]{1,0:T(8,128)(2,1)S(1)} collective-permute-done((bf16[768,128]{1,0:T(8,128)(2,1)}, bf16[768,128]{1,0:T(8,128)(2,1)S(1)}, u32[]{:S(2)}, u32[]{:S(2)}) %collective-permute-start.21) | collective-permute-done | bytes 196640 | tf_op jit(solution)/shard_map/ppermute | solution.py:416
  125.3 2.9 %collective-permute-start.23 = (bf16[384,128]{1,0:T(8,128)(2,1)}, bf16[384,128]{1,0:T(8,128)(2,1)S(1)}, u32[]{:S(2)}, u32[]{:S(2)}) collective-permute-start(bf16[384,128]{1,0:T(8,128)(2,1)} %add_convert_fusion.1), channel_id=1, source_target_pairs={{0,64},{16,80},{32,96},{48,112},{64,0},{80,16},{96,32},{112,48},{1... | collective-permute-start | bytes 294920 | tf_op jit(solution)/shard_map/ppermute | solution.py:416
  131.7 1.8 %shard_map.83.early_hbm = bf16[1024,128]{1,0:T(8,128)(2,1)} custom-call(bf16[8,640,128]{2,1,0:T(8,128)(2,1)S(1)} %all-to-all-done.arrived_ref, bf16[2048,128]{1,0:T(8,128)(2,1)S(1)} %get-tuple-element.19.refs_0_.refs_5_, bf16[2048,128]{1,0:T(8,128)(2,1)S(1)} %collective-permute-done.16.refs_1_.refs_6_, ...), custom_call_target="tpu_custom_call" | custom-call | flops 2000000000 | bytes 4000000 | tf_op jit(solution)/shard_map/pallas_call | solution.py:389
  (74 shorter events, 23.1 us)
Async XLA Ops:
  0.0 10.3 %collective-permute-start.12 = (bf16[1024,128]{1,0:T(8,128)(2,1)}, bf16[1024,128]{1,0:T(8,128)(2,1)S(1)}, u32[]{:S(2)}, u32[]{:S(2)}) collective-permute-start(bf16[1024,128]{1,0:T(8,128)(2,1)} %refs_10_.1), channel_id=1, source_target_pairs={{0,6},{1,7},{2,0},{3,1},{4,2},{5,3},{6,4},{7,5},{8,14},{9,15},{10,... | collective-permute-start | bytes 786440 | tf_op jit(solution)/shard_map/ppermute | solution.py:411
  0.3 10.0 %collective-permute-start.8 = (bf16[1024,128]{1,0:T(8,128)(2,1)}, bf16[1024,128]{1,0:T(8,128)(2,1)S(1)}, u32[]{:S(2)}, u32[]{:S(2)}) collective-permute-start(bf16[1024,128]{1,0:T(8,128)(2,1)} %refs_10_.1), channel_id=1, source_target_pairs={{0,2},{1,3},{2,4},{3,5},{4,6},{5,7},{6,0},{7,1},{8,10},{9,11},{10,... | collective-permute-start | bytes 786440 | tf_op jit(solution)/shard_map/ppermute | solution.py:411
  2.0 9.9 %collective-permute-start.7 = (bf16[1024,128]{1,0:T(8,128)(2,1)}, bf16[1024,128]{1,0:T(8,128)(2,1)S(1)}, u32[]{:S(2)}, u32[]{:S(2)}) collective-permute-start(bf16[1024,128]{1,0:T(8,128)(2,1)} %refs_10_.1), channel_id=1, source_target_pairs={{0,8},{1,9},{2,10},{3,11},{4,12},{5,13},{6,14},{7,15},{8,0},{9,1},... | collective-permute-start | bytes 786440 | tf_op jit(solution)/shard_map/ppermute | solution.py:411
  3.9 14.9 %collective-permute-start.3 = (bf16[1024,128]{1,0:T(8,128)(2,1)}, bf16[1024,128]{1,0:T(8,128)(2,1)S(1)}, u32[]{:S(2)}, u32[]{:S(2)}) collective-permute-start(bf16[1024,128]{1,0:T(8,128)(2,1)} %refs_10_.1), channel_id=1, source_target_pairs={{0,64},{16,80},{32,96},{48,112},{64,0},{80,16},{96,32},{112,48},{1... | collective-permute-start | bytes 786440 | tf_op jit(solution)/shard_map/ppermute | solution.py:416
  7.5 14.8 %collective-permute-start.2 = (bf16[1024,128]{1,0:T(8,128)(2,1)}, bf16[1024,128]{1,0:T(8,128)(2,1)S(1)}, u32[]{:S(2)}, u32[]{:S(2)}) collective-permute-start(bf16[1024,128]{1,0:T(8,128)(2,1)} %refs_10_.1), channel_id=1, source_target_pairs={{0,48},{16,0},{32,16},{48,32},{64,112},{80,64},{96,80},{112,96},{1... | collective-permute-start | bytes 786440 | tf_op jit(solution)/shard_map/ppermute | solution.py:416
  10.3 12.0 %collective-permute-start = (bf16[1024,128]{1,0:T(8,128)(2,1)}, bf16[1024,128]{1,0:T(8,128)(2,1)S(1)}, u32[]{:S(2)}, u32[]{:S(2)}) collective-permute-start(bf16[1024,128]{1,0:T(8,128)(2,1)} %refs_10_.1), channel_id=1, source_target_pairs={{0,16},{16,32},{32,48},{48,0},{64,80},{80,96},{96,112},{112,64},{1... | collective-permute-start | bytes 786440 | tf_op jit(solution)/shard_map/ppermute | solution.py:416
  10.3 14.9 %collective-permute-start.10 = (bf16[1024,128]{1,0:T(8,128)(2,1)S(1)}, bf16[1024,128]{1,0:T(8,128)(2,1)S(1)}, u32[]{:S(2)}, u32[]{:S(2)}) collective-permute-start(bf16[1024,128]{1,0:T(8,128)(2,1)S(1)} %collective-permute-done.8.refs_10_), channel_id=1, source_target_pairs={{0,2},{1,3},{2,4},{3,5},{4,6},{5,7},{6,0},{7,1},{8,10},{9,11},{10,... | collective-permute-start | bytes 786440 | tf_op jit(solution)/shard_map/ppermute | solution.py:411
  11.9 14.0 %collective-permute-start.13 = (bf16[1024,128]{1,0:T(8,128)(2,1)S(1)}, bf16[1024,128]{1,0:T(8,128)(2,1)S(1)}, u32[]{:S(2)}, u32[]{:S(2)}) collective-permute-start(bf16[1024,128]{1,0:T(8,128)(2,1)S(1)} %collective-permute-done.7.refs_9_), channel_id=1, source_target_pairs={{0,6},{1,7},{2,0},{3,1},{4,2},{5,3},{6,4},{7,5},{8,14},{9,15},{10,... | collective-permute-start | bytes 786440 | tf_op jit(solution)/shard_map/ppermute | solution.py:411
  18.8 8.4 %collective-permute-start.11 = (bf16[1024,128]{1,0:T(8,128)(2,1)S(1)}, bf16[1024,128]{1,0:T(8,128)(2,1)S(1)}, u32[]{:S(2)}, u32[]{:S(2)}) collective-permute-start(bf16[1024,128]{1,0:T(8,128)(2,1)S(1)} %collective-permute-done.7.refs_9_), channel_id=1, source_target_pairs={{0,4},{1,5},{2,6},{3,7},{4,0},{5,1},{6,2},{7,3},{8,12},{9,13},{10,... | collective-permute-start | bytes 786440 | tf_op jit(solution)/shard_map/ppermute | solution.py:411
  22.3 10.4 %collective-permute-start.9 = (bf16[1024,128]{1,0:T(8,128)(2,1)S(1)}, bf16[1024,128]{1,0:T(8,128)(2,1)S(1)}, u32[]{:S(2)}, u32[]{:S(2)}) collective-permute-start(bf16[1024,128]{1,0:T(8,128)(2,1)S(1)} %collective-permute-done.7.refs_9_), channel_id=1, source_target_pairs={{0,2},{1,3},{2,4},{3,5},{4,6},{5,7},{6,0},{7,1},{8,10},{9,11},{10,... | collective-permute-start | bytes 786440 | tf_op jit(solution)/shard_map/ppermute | solution.py:411
  22.3 12.3 %collective-permute-start.6 = (bf16[1024,128]{1,0:T(8,128)(2,1)S(1)}, bf16[1024,128]{1,0:T(8,128)(2,1)S(1)}, u32[]{:S(2)}, u32[]{:S(2)}) collective-permute-start(bf16[1024,128]{1,0:T(8,128)(2,1)S(1)} %collective-permute-done.3.refs_4_), channel_id=1, source_target_pairs={{0,48},{16,0},{32,16},{48,32},{64,112},{80,64},{96,80},{112,96},{1... | collective-permute-start | bytes 786440 | tf_op jit(solution)/shard_map/ppermute | solution.py:416
  25.2 10.7 %collective-permute-start.5 = (bf16[1024,128]{1,0:T(8,128)(2,1)S(1)}, bf16[1024,128]{1,0:T(8,128)(2,1)S(1)}, u32[]{:S(2)}, u32[]{:S(2)}) collective-permute-start(bf16[1024,128]{1,0:T(8,128)(2,1)S(1)} %collective-permute-done.3.refs_4_), channel_id=1, source_target_pairs={{0,32},{16,48},{32,0},{48,16},{64,96},{80,112},{96,64},{112,80},{1... | collective-permute-start | bytes 786440 | tf_op jit(solution)/shard_map/ppermute | solution.py:416
  26.0 12.9 %collective-permute-start.4 = (bf16[1024,128]{1,0:T(8,128)(2,1)S(1)}, bf16[1024,128]{1,0:T(8,128)(2,1)S(1)}, u32[]{:S(2)}, u32[]{:S(2)}) collective-permute-start(bf16[1024,128]{1,0:T(8,128)(2,1)S(1)} %collective-permute-done.3.refs_4_), channel_id=1, source_target_pairs={{0,16},{16,32},{32,48},{48,0},{64,80},{80,96},{96,112},{112,64},{1... | collective-permute-start | bytes 786440 | tf_op jit(solution)/shard_map/ppermute | solution.py:416
  27.2 16.9 %collective-permute-start.1 = (bf16[1024,128]{1,0:T(8,128)(2,1)S(1)}, bf16[1024,128]{1,0:T(8,128)(2,1)}, u32[]{:S(2)}, u32[]{:S(2)}) collective-permute-start(bf16[1024,128]{1,0:T(8,128)(2,1)S(1)} %collective-permute-done.refs_1_), channel_id=1, source_target_pairs={{0,16},{16,32},{32,48},{48,0},{64,80},{80,96},{96,112},{112,64},{1... | collective-permute-start | bytes 786440 | tf_op jit(solution)/shard_map/ppermute | solution.py:416
  66.5 12.6 %collective-permute-start.14 = (bf16[8192,128]{1,0:T(8,128)(2,1)}, bf16[8192,128]{1,0:T(8,128)(2,1)}, u32[]{:S(2)}, u32[]{:S(2)}) collective-permute-start(bf16[8192,128]{1,0:T(8,128)(2,1)} %get-tuple-element.16.refs_2_), channel_id=1, source_target_pairs={{0,1},{1,0},{2,3},{3,2},{4,5},{5,4},{6,7},{7,6},{8,9},{9,8},{10,11... | collective-permute-start | bytes 6291464 | tf_op jit(solution)/shard_map/ppermute | solution.py:420
  75.1 39.6 %collective-permute-start.16 = (bf16[2048,128]{1,0:T(8,128)(2,1)}, bf16[2048,128]{1,0:T(8,128)(2,1)S(1)}, u32[]{:S(2)}, u32[]{:S(2)}) collective-permute-start(bf16[2048,128]{1,0:T(8,128)(2,1)} %get-tuple-element.20), channel_id=1, source_target_pairs={{0,2},{1,3},{2,4},{3,5},{4,6},{5,7},{6,0},{7,1},{8,10},{9,11},{10,... | collective-permute-start | bytes 1572872 | tf_op jit(solution)/shard_map/ppermute | solution.py:411
  75.2 39.7 %collective-permute-start.17 = (bf16[2048,128]{1,0:T(8,128)(2,1)}, bf16[2048,128]{1,0:T(8,128)(2,1)S(1)}, u32[]{:S(2)}, u32[]{:S(2)}) collective-permute-start(bf16[2048,128]{1,0:T(8,128)(2,1)} %get-tuple-element.21), channel_id=1, source_target_pairs={{0,6},{1,7},{2,0},{3,1},{4,2},{5,3},{6,4},{7,5},{8,14},{9,15},{10,... | collective-permute-start | bytes 1572872 | tf_op jit(solution)/shard_map/ppermute | solution.py:411
  77.2 37.7 %collective-permute-start.18 = (bf16[2048,128]{1,0:T(8,128)(2,1)}, bf16[2048,128]{1,0:T(8,128)(2,1)S(1)}, u32[]{:S(2)}, u32[]{:S(2)}) collective-permute-start(bf16[2048,128]{1,0:T(8,128)(2,1)} %get-tuple-element.22), channel_id=1, source_target_pairs={{0,4},{1,5},{2,6},{3,7},{4,0},{5,1},{6,2},{7,3},{8,12},{9,13},{10,... | collective-permute-start | bytes 1572872 | tf_op jit(solution)/shard_map/ppermute | solution.py:411
  95.1 33.8 %all-to-all-start = ((bf16[8,640,128]{2,1,0:T(8,128)(2,1)}), bf16[8,640,128]{2,1,0:T(8,128)(2,1)S(1)}, u32[]{:S(2)}, u32[]{:S(2)}) async-start(bf16[8,640,128]{2,1,0:T(8,128)(2,1)} %bitcast.13), calls=%async_computation | async-start | bytes 2621440 | tf_op jit(solution)/shard_map/all_to_all | solution.py:424
  111.4 8.9 %collective-permute-start.20 = (bf16[768,128]{1,0:T(8,128)(2,1)}, bf16[768,128]{1,0:T(8,128)(2,1)S(1)}, u32[]{:S(2)}, u32[]{:S(2)}) collective-permute-start(bf16[768,128]{1,0:T(8,128)(2,1)} %get-tuple-element.24), channel_id=1, source_target_pairs={{0,16},{16,32},{32,48},{48,0},{64,80},{80,96},{96,112},{112,64},{1... | collective-permute-start | bytes 589832 | tf_op jit(solution)/shard_map/ppermute | solution.py:416
  111.5 10.8 %collective-permute-start.21 = (bf16[768,128]{1,0:T(8,128)(2,1)}, bf16[768,128]{1,0:T(8,128)(2,1)S(1)}, u32[]{:S(2)}, u32[]{:S(2)}) collective-permute-start(bf16[768,128]{1,0:T(8,128)(2,1)} %get-tuple-element.25), channel_id=1, source_target_pairs={{0,48},{16,0},{32,16},{48,32},{64,112},{80,64},{96,80},{112,96},{1... | collective-permute-start | bytes 589832 | tf_op jit(solution)/shard_map/ppermute | solution.py:416
  114.7 8.3 %collective-permute-start.22 = (bf16[768,128]{1,0:T(8,128)(2,1)}, bf16[768,128]{1,0:T(8,128)(2,1)S(1)}, u32[]{:S(2)}, u32[]{:S(2)}) collective-permute-start(bf16[768,128]{1,0:T(8,128)(2,1)} %get-tuple-element.26), channel_id=1, source_target_pairs={{0,32},{16,48},{32,0},{48,16},{64,96},{80,112},{96,64},{112,80},{1... | collective-permute-start | bytes 589832 | tf_op jit(solution)/shard_map/ppermute | solution.py:416
  115.0 13.1 %collective-permute-start.19 = (bf16[1024,128]{1,0:T(8,128)(2,1)S(1)}, bf16[1024,128]{1,0:T(8,128)(2,1)S(1)}, u32[]{:S(2)}, u32[]{:S(2)}) collective-permute-start(bf16[1024,128]{1,0:T(8,128)(2,1)S(1)} %add_convert_fusion), channel_id=1, source_target_pairs={{0,8},{1,9},{2,10},{3,11},{4,12},{5,13},{6,14},{7,15},{8,0},{9,1},... | collective-permute-start | bytes 786440 | tf_op jit(solution)/shard_map/ppermute | solution.py:411
  125.3 8.2 %collective-permute-start.23 = (bf16[384,128]{1,0:T(8,128)(2,1)}, bf16[384,128]{1,0:T(8,128)(2,1)S(1)}, u32[]{:S(2)}, u32[]{:S(2)}) collective-permute-start(bf16[384,128]{1,0:T(8,128)(2,1)} %add_convert_fusion.1), channel_id=1, source_target_pairs={{0,64},{16,80},{32,96},{48,112},{64,0},{80,16},{96,32},{112,48},{1... | collective-permute-start | bytes 294920 | tf_op jit(solution)/shard_map/ppermute | solution.py:416
  (18 other events, 129.1 us)
where the time goes:
time: 138 us; the launch traced here: 135 us
  Pallas kernels  56 us (41%)
  starting transfers between devices  37 us (27%)
  waiting for transfers between devices  29 us (21%)
  local copies, waits for them, and re-layouts  10.2 us (7%)
  other arithmetic  2.48 us (2%)
    pallas_call x2, Pallas kernels, tower_messages(): pl.pallas_call(lambda *refs: tower_kernel(part, *refs), out_shape=[jax.Sh...  28.5 us
    ppermute x11, waiting for transfers between devices, along_row(): return lax.ppermute(value, 'row', pairs)  25.2 us
    pallas_call x1, Pallas kernels, plate_messages(): pl.pallas_call(plate_kernel, out_shape=(half, half, half), in_specs=[SMEM...  21.4 us
    ppermute x11, starting transfers between devices, along_row(): return lax.ppermute(value, 'row', pairs)  18.7 us
    ppermute x11, starting transfers between devices, along_col(): return lax.ppermute(value, 'col', pairs)  14 us
    unnamed x36, local copies, waits for them, and re-layouts  9.04 us
    all_to_all x1, starting transfers between devices, over_rows(): lax.all_to_all(part.reshape(8, -1, D), 'row', split_axis=0, concat_axis=0...  3.76 us
    pallas_call x2, Pallas kernels, update(): pl.pallas_call(early_kernel if part == 0 else late_kernel, out_shape=jax....  3.25 us
  transfers between devices with their start and end apart: 25, of which 11 were waited for; matrix products, arithmetic and copies ran while one was open for 5% of the time, Pallas kernels for 25%

commit v1 on v0

--- a/solution.py
+++ b/solution.py
@@ -12,7 +12,7 @@
 SLOTS = 128
 BLOCK = 8
 HOME = 8
-CUT = 5
+CUT = 4
 MIB = 1024 * 1024
 
 
@@ -128,7 +128,7 @@
 
 
 def tower_kernel(part, index_ref, bins_hbm, mine_hbm, theirs_hbm, weight_ref, *refs):
-    out_refs = refs[: 1 if part == 0 else 4]
+    out_refs = refs[: 1 if part == 0 else 8]
     bins_ref, plate_ref, acc_ref, near_a, near_b, slot_ref, from_ref, to_ref, sems, plate_sems = refs[len(out_refs) :]
     col = index_ref[1, SLOTS]
     col_z, col_y, core = col // 8, (col // 2) % 4, col % 2
@@ -227,9 +227,9 @@
     row = index_ref[0, SLOTS]
     for j in range(8):
         home = j if part == 0 else ((row // 4 + j // 4) % 2) * 4 + (row % 4 + j % 4) % 4
-        out_ref = out_refs[0 if part == 0 else j % 4]
+        out_ref = out_refs[0 if part == 0 else j]
         for u in range(width):
-            at = ((j if part == 0 else j // 4) * width + u) * CLUSTER
+            at = ((j * width if part == 0 else 0) + u) * CLUSTER
             out_ref[at : at + CLUSTER, :] = acc_ref[home * width + u].astype(jnp.bfloat16)
 
 
@@ -290,13 +290,13 @@
 
 
 def late_kernel(early_hbm, *refs):
-    arrived_refs, side_refs, refs = refs[:5], refs[5:10], refs[10:]
+    arrived_refs, side_refs, refs = refs[:8], refs[8:13], refs[13:]
     features_ref, gain_ref, in_ref, last_ref, out_hbm, out_ref, sem = refs
     for c in range(HOME - CUT):
         at = slice(c * CLUSTER, (c + 1) * CLUSTER)
         rows = slice((CUT + c) * CLUSTER, (CUT + c + 1) * CLUSTER)
         flipped = arrived_refs[0][at, :].astype(jnp.float32)
-        for r in range(1, 5):
+        for r in range(1, 8):
             flipped += arrived_refs[r][at, :].astype(jnp.float32)
         out_ref[at, :] = updated_rows(flipped, rows, side_refs, features_ref, gain_ref, in_ref, last_ref)
     copy = pltpu.make_async_copy(out_ref, out_hbm.at[pl.ds(CUT * CLUSTER, (HOME - CUT) * CLUSTER)], sem)
@@ -341,7 +341,7 @@
 
 def tower_messages(part, pair_index, bins, mine, theirs, weight):
     clusters = 8 * (CUT if part == 0 else HOME - CUT)
-    outs = 1 if part == 0 else 4
+    outs = 1 if part == 0 else 8
     near = pltpu.VMEM((BLOCK // 4, BINS * D, 2 * CLUSTER), jnp.bfloat16)
     return pl.pallas_call(
         lambda *refs: tower_kernel(part, *refs),
@@ -390,7 +390,8 @@
         early_kernel if part == 0 else late_kernel,
         out_shape=jax.ShapeDtypeStruct((1024, D), jnp.bfloat16),
         grid=(1,),
-        in_specs=([HBM] + [pl.BlockSpec((rows, D), lambda i: (0, 0))] * 5 if part else [VMEM])
+        in_specs=[HBM] * part
+        + [VMEM] * (1 if part == 0 else 8)
         + [pl.BlockSpec((1024, D), lambda i: (0, 0))] * 4
         + [VMEM] * 5,
         out_specs=HBM,
@@ -455,13 +456,7 @@
     back = [along_col(sums[d - 1], 0, d) for d in (1, 3, 2)]
     second = tower_messages(1, table, bins, plate_mine, plate_theirs, tower_flip)
     first_back = over_rows(first[0])
-    second_back = [along_row(second[d], 0, d) for d in (1, 3, 2)]
-    half = (HOME - CUT) * CLUSTER
-    second_far = second[0][half:].astype(jnp.float32)
-    for part in second_back:
-        second_far = second_far + part[half:].astype(jnp.float32)
-    second_far = second_far.astype(jnp.bfloat16)
-    second_far = along_row(second_far, 1, 0)
+    second_back = [along_row(second[j], j // 4, j % 4) for j in (6, 5, 7, 4, 2, 1, 3)]
     far = own[1024:].astype(jnp.float32)
     for part in back:
         far = far + part[1024:].astype(jnp.float32)
@@ -469,7 +464,7 @@
     across = along_col(far, 1, 0)
     rest = ([own, *back], across, features, norm_gain.reshape(1, D), update_in, update_out)
     early = update(0, [first_back], *rest)
-    return update(1, [early, second[0], *second_back, second_far], *rest)
+    return update(1, [early, second[0], *second_back], *rest)
 
 
 def solution(mesh):

time: 138 us -> 142 us (1.029)
  the two profiles are of different devices: /device:TPU:8 before, /device:TPU:56 now
where the time goes in v1:
time: 142 us
  starting transfers between devices  70.4 us (50%)
  Pallas kernels  34.3 us (24%)
  waiting for transfers between devices  25.2 us (18%)
  local copies, waits for them, and re-layouts  10 us (7%)
  other arithmetic  1.6 us (1%)
    ppermute x14, starting transfers between devices, along_row(): return lax.ppermute(value, 'row', pairs)  40.9 us
    ppermute x11, starting transfers between devices, along_col(): return lax.ppermute(value, 'col', pairs)  18.4 us
    ppermute x11, waiting for transfers between devices, along_col(): return lax.ppermute(value, 'col', pairs)  15.4 us
    pallas_call x2, Pallas kernels, tower_messages(): pl.pallas_call(lambda *refs: tower_kernel(part, *refs), out_shape=[jax.Sh...  14.2 us
    pallas_call x1, Pallas kernels, plate_messages(): pl.pallas_call(plate_kernel, out_shape=(half, half, half), in_specs=[SMEM...  12.8 us
    all_to_all x1, starting transfers between devices, over_rows(): lax.all_to_all(part.reshape(8, -1, D), 'row', split_axis=0, concat_axis=0...  10.5 us
    unnamed x28, local copies, waits for them, and re-layouts  8.8 us
    ppermute x14, waiting for transfers between devices, along_row(): return lax.ppermute(value, 'row', pairs)  7.72 us
  transfers between devices with their start and end apart: 28, of which 8 were waited for; matrix products, arithmetic and copies ran while one was open for 4% of the time, Pallas kernels for 13%

profile of v1, /device:TPU:56, one launch (start us, length us, event | category | flops | bytes accessed | tf_op | source)
XLA Modules:
  0.0 141.9 jit_solution(6266337539902427792)
XLA Ops:
  0.1 3.3 %collective-permute-start.3 = (bf16[1024,128]{1,0:T(8,128)(2,1)}, bf16[1024,128]{1,0:T(8,128)(2,1)S(1)}, u32[]{:S(2)}, u32[]{:S(2)}) collective-permute-start(bf16[1024,128]{1,0:T(8,128)(2,1)} %refs_13_.1), channel_id=1, source_target_pairs={{0,64},{16,80},{32,96},{48,112},{64,0},{80,16},{96,32},{112,48},{1... | collective-permute-start | bytes 786440 | tf_op jit(solution)/shard_map/ppermute | solution.py:417
  5.1 1.8 %collective-permute-start.12 = (bf16[1024,128]{1,0:T(8,128)(2,1)}, bf16[1024,128]{1,0:T(8,128)(2,1)S(1)}, u32[]{:S(2)}, u32[]{:S(2)}) collective-permute-start(bf16[1024,128]{1,0:T(8,128)(2,1)} %refs_13_.1), channel_id=1, source_target_pairs={{0,6},{1,7},{2,0},{3,1},{4,2},{5,3},{6,4},{7,5},{8,14},{9,15},{10,... | collective-permute-start | bytes 786440 | tf_op jit(solution)/shard_map/ppermute | solution.py:412
  6.9 2.5 %collective-permute-done.7.refs_9_ = bf16[1024,128]{1,0:T(8,128)(2,1)S(1)} collective-permute-done((bf16[1024,128]{1,0:T(8,128)(2,1)}, bf16[1024,128]{1,0:T(8,128)(2,1)S(1)}, u32[]{:S(2)}, u32[]{:S(2)}) %collective-permute-start.7) | collective-permute-done | bytes 262176 | tf_op jit(solution)/shard_map/ppermute | solution.py:412
  9.4 2.8 %collective-permute-start.2 = (bf16[1024,128]{1,0:T(8,128)(2,1)}, bf16[1024,128]{1,0:T(8,128)(2,1)S(1)}, u32[]{:S(2)}, u32[]{:S(2)}) collective-permute-start(bf16[1024,128]{1,0:T(8,128)(2,1)} %refs_13_.1), channel_id=1, source_target_pairs={{0,48},{16,0},{32,16},{48,32},{64,112},{80,64},{96,80},{112,96},{1... | collective-permute-start | bytes 786440 | tf_op jit(solution)/shard_map/ppermute | solution.py:417
  12.1 3.1 %collective-permute-done.3.refs_4_ = bf16[1024,128]{1,0:T(8,128)(2,1)S(1)} collective-permute-done((bf16[1024,128]{1,0:T(8,128)(2,1)}, bf16[1024,128]{1,0:T(8,128)(2,1)S(1)}, u32[]{:S(2)}, u32[]{:S(2)}) %collective-permute-start.3) | collective-permute-done | bytes 262176 | tf_op jit(solution)/shard_map/ppermute | solution.py:417
  18.0 2.7 %collective-permute-start.5 = (bf16[1024,128]{1,0:T(8,128)(2,1)S(1)}, bf16[1024,128]{1,0:T(8,128)(2,1)S(1)}, u32[]{:S(2)}, u32[]{:S(2)}) collective-permute-start(bf16[1024,128]{1,0:T(8,128)(2,1)S(1)} %collective-permute-done.3.refs_4_), channel_id=1, source_target_pairs={{0,32},{16,48},{32,0},{48,16},{64,96},{80,112},{96,64},{112,80},{1... | collective-permute-start | bytes 786440 | tf_op jit(solution)/shard_map/ppermute | solution.py:417
  22.2 3.7 %collective-permute-done.11.refs_13_ = bf16[1024,128]{1,0:T(8,128)(2,1)S(1)} collective-permute-done((bf16[1024,128]{1,0:T(8,128)(2,1)S(1)}, bf16[1024,128]{1,0:T(8,128)(2,1)S(1)}, u32[]{:S(2)}, u32[]{:S(2)}) %collective-permute-start.11) | collective-permute-done | bytes 262176 | tf_op jit(solution)/shard_map/ppermute | solution.py:412
  26.0 3.6 %collective-permute-done.13.refs_15_ = bf16[1024,128]{1,0:T(8,128)(2,1)S(1)} collective-permute-done((bf16[1024,128]{1,0:T(8,128)(2,1)S(1)}, bf16[1024,128]{1,0:T(8,128)(2,1)S(1)}, u32[]{:S(2)}, u32[]{:S(2)}) %collective-permute-start.13) | collective-permute-done | bytes 262176 | tf_op jit(solution)/shard_map/ppermute | solution.py:412
  34.4 4.6 %collective-permute-done.1.refs_2_ = bf16[1024,128]{1,0:T(8,128)(2,1)S(1)} collective-permute-done((bf16[1024,128]{1,0:T(8,128)(2,1)S(1)}, bf16[1024,128]{1,0:T(8,128)(2,1)S(1)}, u32[]{:S(2)}, u32[]{:S(2)}) %collective-permute-start.1) | collective-permute-done | bytes 262176 | tf_op jit(solution)/shard_map/ppermute | solution.py:417
  40.0 12.8 %plate_messages.1 = (bf16[8192,128]{1,0:T(8,128)(2,1)}, bf16[8192,128]{1,0:T(8,128)(2,1)}, bf16[8192,128]{1,0:T(8,128)(2,1)}) custom-call(s32[2,256]{1,0:T(2,128)S(1)} %pad_add_fusion.index_ref.refs_0_, s32[128,128,128]{2,1,0:T(8,128)} %refs_1_.3, bf16[1024,128]{1,0:T(8,128)(2,1)S(1)} %copy-done.1, bf16[1024,128]{1,0:T(8,128)(2,1)S(1)} %collective-permute-done.refs_1_, ...), custom_call_target="tpu_custom_call" | custom-call | flops 24999999488 | bytes 15000000 | tf_op jit(solution)/shard_map/plate_messages/pallas_call | solution.py:319
  55.3 2.1 %collective-permute-done.15.theirs_hbm = bf16[8192,128]{1,0:T(8,128)(2,1)S(1)} collective-permute-done((bf16[8192,128]{1,0:T(8,128)(2,1)}, bf16[8192,128]{1,0:T(8,128)(2,1)S(1)}, u32[]{:S(2)}, u32[]{:S(2)}) %collective-permute-start.15) | collective-permute-done | bytes 2097184 | tf_op jit(solution)/shard_map/ppermute | solution.py:421
  58.7 2.9 %core_sum.1 = (bf16[2048,128]{1,0:T(8,128)(2,1)S(1)}, bf16[2048,128]{1,0:T(8,128)(2,1)}, bf16[2048,128]{1,0:T(8,128)(2,1)}, bf16[2048,128]{1,0:T(8,128)(2,1)}) custom-call(bf16[8192,128]{1,0:T(8,128)(2,1)} %get-tuple-element.21.mine_hbm, bf16[8192,128]{1,0:T(8,128)(2,1)} %copy-done.12), custom_call_target="tpu_custom_call" | custom-call | flops 2000000000 | bytes 6000000 | tf_op jit(solution)/shard_map/core_sum/pallas_call | solution.py:369
  61.6 2.3 %collective-permute-start.16 = (bf16[2048,128]{1,0:T(8,128)(2,1)}, bf16[2048,128]{1,0:T(8,128)(2,1)S(1)}, u32[]{:S(2)}, u32[]{:S(2)}) collective-permute-start(bf16[2048,128]{1,0:T(8,128)(2,1)} %get-tuple-element.24), channel_id=1, source_target_pairs={{0,2},{1,3},{2,4},{3,5},{4,6},{5,7},{6,0},{7,1},{8,10},{9,11},{10,... | collective-permute-start | bytes 1572872 | tf_op jit(solution)/shard_map/ppermute | solution.py:412
  63.9 9.6 %collective-permute-start.18 = (bf16[2048,128]{1,0:T(8,128)(2,1)}, bf16[2048,128]{1,0:T(8,128)(2,1)S(1)}, u32[]{:S(2)}, u32[]{:S(2)}) collective-permute-start(bf16[2048,128]{1,0:T(8,128)(2,1)} %get-tuple-element.26), channel_id=1, source_target_pairs={{0,4},{1,5},{2,6},{3,7},{4,0},{5,1},{6,2},{7,3},{8,12},{9,13},{10,... | collective-permute-start | bytes 1572872 | tf_op jit(solution)/shard_map/ppermute | solution.py:412
  73.5 7.1 %shard_map.82 = bf16[4096,128]{1,0:T(8,128)(2,1)} custom-call(s32[2,256]{1,0:T(2,128)} %copy-done, s32[128,128,128]{2,1,0:T(8,128)} %refs_1_.3, bf16[8192,128]{1,0:T(8,128)(2,1)} %get-tuple-element.20.refs_2_, bf16[8192,128]{1,0:T(8,128)(2,1)} %collective-permute-done.14.refs_3_, bf16[128,1024]{1,0:T(8,128)(2,1)} %bitcast.16), custom_call_target="tpu_custom_call" | custom-call | flops 15000000512 | bytes 10000000 | tf_op jit(solution)/shard_map/pallas_call | solution.py:346
  80.6 10.5 %all-to-all-start = ((bf16[8,512,128]{2,1,0:T(8,128)(2,1)}), bf16[8,512,128]{2,1,0:T(8,128)(2,1)S(1)}, u32[]{:S(2)}, u32[]{:S(2)}) async-start(bf16[8,512,128]{2,1,0:T(8,128)(2,1)} %bitcast.13), calls=%async_computation | async-start | bytes 2097152 | tf_op jit(solution)/shard_map/all_to_all | solution.py:425
  91.1 5.5 %collective-permute-done.18.refs_3_.refs_11_ = bf16[2048,128]{1,0:T(8,128)(2,1)S(1)} collective-permute-done((bf16[2048,128]{1,0:T(8,128)(2,1)}, bf16[2048,128]{1,0:T(8,128)(2,1)S(1)}, u32[]{:S(2)}, u32[]{:S(2)}) %collective-permute-start.18) | collective-permute-done | bytes 524320 | tf_op jit(solution)/shard_map/ppermute | solution.py:412
  97.4 2.6 %collective-permute-start.19 = (bf16[1024,128]{1,0:T(8,128)(2,1)}, bf16[1024,128]{1,0:T(8,128)(2,1)S(1)}, u32[]{:S(2)}, u32[]{:S(2)}) collective-permute-start(bf16[1024,128]{1,0:T(8,128)(2,1)} %add_convert_fusion), channel_id=1, source_target_pairs={{0,8},{1,9},{2,10},{3,11},{4,12},{5,13},{6,14},{7,15},{8,0},{9,1},... | collective-permute-start | bytes 786440 | tf_op jit(solution)/shard_map/ppermute | solution.py:412
  100.0 7.0 %shard_map.84 = (bf16[512,128]{1,0:T(8,128)(2,1)}, bf16[512,128]{1,0:T(8,128)(2,1)}, bf16[512,128]{1,0:T(8,128)(2,1)}, bf16[512,128]{1,0:T(8,128)(2,1)}, bf16[51...) custom-call(s32[2,256]{1,0:T(2,128)} %copy-done, ...), custom_call_target="tpu_custom_call" | custom-call | flops 15000000512 | bytes 10000000 | tf_op jit(solution)/shard_map/pallas_call | solution.py:346
  108.7 5.6 %collective-permute-start.21 = (bf16[512,128]{1,0:T(8,128)(2,1)}, bf16[512,128]{1,0:T(8,128)(2,1)S(1)}, u32[]{:S(2)}, u32[]{:S(2)}) collective-permute-start(bf16[512,128]{1,0:T(8,128)(2,1)} %get-tuple-element.29), channel_id=1, source_target_pairs={{0,80},{16,96},{32,112},{48,64},{64,16},{80,32},{96,48},{112,0},{1... | collective-permute-start | bytes 393224 | tf_op jit(solution)/shard_map/ppermute | solution.py:417
  115.9 11.4 %collective-permute-start.23 = (bf16[512,128]{1,0:T(8,128)(2,1)}, bf16[512,128]{1,0:T(8,128)(2,1)}, u32[]{:S(2)}, u32[]{:S(2)}) collective-permute-start(bf16[512,128]{1,0:T(8,128)(2,1)} %get-tuple-element.31), channel_id=1, source_target_pairs={{0,64},{16,80},{32,96},{48,112},{64,0},{80,16},{96,32},{112,48},{1... | collective-permute-start | bytes 393224 | tf_op jit(solution)/shard_map/ppermute | solution.py:417
  127.3 2.7 %collective-permute-start.24 = (bf16[512,128]{1,0:T(8,128)(2,1)}, bf16[512,128]{1,0:T(8,128)(2,1)}, u32[]{:S(2)}, u32[]{:S(2)}) collective-permute-start(bf16[512,128]{1,0:T(8,128)(2,1)} %get-tuple-element.32), channel_id=1, source_target_pairs={{0,32},{16,48},{32,0},{48,16},{64,96},{80,112},{96,64},{112,80},{1... | collective-permute-start | bytes 393224 | tf_op jit(solution)/shard_map/ppermute | solution.py:417
  131.4 3.2 %collective-permute-start.26 = (bf16[512,128]{1,0:T(8,128)(2,1)}, bf16[512,128]{1,0:T(8,128)(2,1)}, u32[]{:S(2)}, u32[]{:S(2)}) collective-permute-start(bf16[512,128]{1,0:T(8,128)(2,1)} %get-tuple-element.34), channel_id=1, source_target_pairs={{0,48},{16,0},{32,16},{48,32},{64,112},{80,64},{96,80},{112,96},{1... | collective-permute-start | bytes 393224 | tf_op jit(solution)/shard_map/ppermute | solution.py:417
  138.9 2.8 %shard_map.85 = bf16[1024,128]{1,0:T(8,128)(2,1)} custom-call(bf16[1024,128]{1,0:T(8,128)(2,1)} %shard_map.83.early_hbm, bf16[512,128]{1,0:T(8,128)(2,1)S(1)} %copy-done.11, bf16[512,128]{1,0:T(8,128)(2,1)S(1)} %collective-permute-done.20.refs_1_, bf16[512,128]{1,0:T(8,128)(2,1)S(1)} %copy-done.6, ...), custom_call_target="tpu_custom_call", output_to_operand_aliasing={{}: (0, {})} | custom-call | flops 2000000000 | bytes 4000000 | tf_op jit(solution)/shard_map/pallas_call | solution.py:389
  (71 shorter events, 25.3 us)
Async XLA Ops:
  0.0 9.4 %collective-permute-start.7 = (bf16[1024,128]{1,0:T(8,128)(2,1)}, bf16[1024,128]{1,0:T(8,128)(2,1)S(1)}, u32[]{:S(2)}, u32[]{:S(2)}) collective-permute-start(bf16[1024,128]{1,0:T(8,128)(2,1)} %refs_13_.1), channel_id=1, source_target_pairs={{0,8},{1,9},{2,10},{3,11},{4,12},{5,13},{6,14},{7,15},{8,0},{9,1},... | collective-permute-start | bytes 786440 | tf_op jit(solution)/shard_map/ppermute | solution.py:412
  0.1 15.1 %collective-permute-start.3 = (bf16[1024,128]{1,0:T(8,128)(2,1)}, bf16[1024,128]{1,0:T(8,128)(2,1)S(1)}, u32[]{:S(2)}, u32[]{:S(2)}) collective-permute-start(bf16[1024,128]{1,0:T(8,128)(2,1)} %refs_13_.1), channel_id=1, source_target_pairs={{0,64},{16,80},{32,96},{48,112},{64,0},{80,16},{96,32},{112,48},{1... | collective-permute-start | bytes 786440 | tf_op jit(solution)/shard_map/ppermute | solution.py:417
  3.4 13.1 %collective-permute-start = (bf16[1024,128]{1,0:T(8,128)(2,1)}, bf16[1024,128]{1,0:T(8,128)(2,1)S(1)}, u32[]{:S(2)}, u32[]{:S(2)}) collective-permute-start(bf16[1024,128]{1,0:T(8,128)(2,1)} %refs_13_.1), channel_id=1, source_target_pairs={{0,16},{16,32},{32,48},{48,0},{64,80},{80,96},{96,112},{112,64},{1... | collective-permute-start | bytes 786440 | tf_op jit(solution)/shard_map/ppermute | solution.py:417
  4.9 11.6 %collective-permute-start.8 = (bf16[1024,128]{1,0:T(8,128)(2,1)}, bf16[1024,128]{1,0:T(8,128)(2,1)S(1)}, u32[]{:S(2)}, u32[]{:S(2)}) collective-permute-start(bf16[1024,128]{1,0:T(8,128)(2,1)} %refs_13_.1), channel_id=1, source_target_pairs={{0,2},{1,3},{2,4},{3,5},{4,6},{5,7},{6,0},{7,1},{8,10},{9,11},{10,... | collective-permute-start | bytes 786440 | tf_op jit(solution)/shard_map/ppermute | solution.py:412
  5.1 12.9 %collective-permute-start.12 = (bf16[1024,128]{1,0:T(8,128)(2,1)}, bf16[1024,128]{1,0:T(8,128)(2,1)S(1)}, u32[]{:S(2)}, u32[]{:S(2)}) collective-permute-start(bf16[1024,128]{1,0:T(8,128)(2,1)} %refs_13_.1), channel_id=1, source_target_pairs={{0,6},{1,7},{2,0},{3,1},{4,2},{5,3},{6,4},{7,5},{8,14},{9,15},{10,... | collective-permute-start | bytes 786440 | tf_op jit(solution)/shard_map/ppermute | solution.py:412
  9.4 11.4 %collective-permute-start.2 = (bf16[1024,128]{1,0:T(8,128)(2,1)}, bf16[1024,128]{1,0:T(8,128)(2,1)S(1)}, u32[]{:S(2)}, u32[]{:S(2)}) collective-permute-start(bf16[1024,128]{1,0:T(8,128)(2,1)} %refs_13_.1), channel_id=1, source_target_pairs={{0,48},{16,0},{32,16},{48,32},{64,112},{80,64},{96,80},{112,96},{1... | collective-permute-start | bytes 786440 | tf_op jit(solution)/shard_map/ppermute | solution.py:417
  15.2 10.7 %collective-permute-start.11 = (bf16[1024,128]{1,0:T(8,128)(2,1)S(1)}, bf16[1024,128]{1,0:T(8,128)(2,1)S(1)}, u32[]{:S(2)}, u32[]{:S(2)}) collective-permute-start(bf16[1024,128]{1,0:T(8,128)(2,1)S(1)} %collective-permute-done.7.refs_9_), channel_id=1, source_target_pairs={{0,4},{1,5},{2,6},{3,7},{4,0},{5,1},{6,2},{7,3},{8,12},{9,13},{10,... | collective-permute-start | bytes 786440 | tf_op jit(solution)/shard_map/ppermute | solution.py:412
  16.5 13.1 %collective-permute-start.13 = (bf16[1024,128]{1,0:T(8,128)(2,1)S(1)}, bf16[1024,128]{1,0:T(8,128)(2,1)S(1)}, u32[]{:S(2)}, u32[]{:S(2)}) collective-permute-start(bf16[1024,128]{1,0:T(8,128)(2,1)S(1)} %collective-permute-done.7.refs_9_), channel_id=1, source_target_pairs={{0,6},{1,7},{2,0},{3,1},{4,2},{5,3},{6,4},{7,5},{8,14},{9,15},{10,... | collective-permute-start | bytes 786440 | tf_op jit(solution)/shard_map/ppermute | solution.py:412
  16.5 14.6 %collective-permute-start.4 = (bf16[1024,128]{1,0:T(8,128)(2,1)S(1)}, bf16[1024,128]{1,0:T(8,128)(2,1)S(1)}, u32[]{:S(2)}, u32[]{:S(2)}) collective-permute-start(bf16[1024,128]{1,0:T(8,128)(2,1)S(1)} %collective-permute-done.3.refs_4_), channel_id=1, source_target_pairs={{0,16},{16,32},{32,48},{48,0},{64,80},{80,96},{96,112},{112,64},{1... | collective-permute-start | bytes 786440 | tf_op jit(solution)/shard_map/ppermute | solution.py:417
  18.0 16.3 %collective-permute-start.5 = (bf16[1024,128]{1,0:T(8,128)(2,1)S(1)}, bf16[1024,128]{1,0:T(8,128)(2,1)S(1)}, u32[]{:S(2)}, u32[]{:S(2)}) collective-permute-start(bf16[1024,128]{1,0:T(8,128)(2,1)S(1)} %collective-permute-done.3.refs_4_), channel_id=1, source_target_pairs={{0,32},{16,48},{32,0},{48,16},{64,96},{80,112},{96,64},{112,80},{1... | collective-permute-start | bytes 786440 | tf_op jit(solution)/shard_map/ppermute | solution.py:417
  20.8 13.6 %collective-permute-start.6 = (bf16[1024,128]{1,0:T(8,128)(2,1)S(1)}, bf16[1024,128]{1,0:T(8,128)(2,1)S(1)}, u32[]{:S(2)}, u32[]{:S(2)}) collective-permute-start(bf16[1024,128]{1,0:T(8,128)(2,1)S(1)} %collective-permute-done.3.refs_4_), channel_id=1, source_target_pairs={{0,48},{16,0},{32,16},{48,32},{64,112},{80,64},{96,80},{112,96},{1... | collective-permute-start | bytes 786440 | tf_op jit(solution)/shard_map/ppermute | solution.py:417
  26.0 8.4 %collective-permute-start.9 = (bf16[1024,128]{1,0:T(8,128)(2,1)S(1)}, bf16[1024,128]{1,0:T(8,128)(2,1)S(1)}, u32[]{:S(2)}, u32[]{:S(2)}) collective-permute-start(bf16[1024,128]{1,0:T(8,128)(2,1)S(1)} %collective-permute-done.7.refs_9_), channel_id=1, source_target_pairs={{0,2},{1,3},{2,4},{3,5},{4,6},{5,7},{6,0},{7,1},{8,10},{9,11},{10,... | collective-permute-start | bytes 786440 | tf_op jit(solution)/shard_map/ppermute | solution.py:412
  29.5 9.4 %collective-permute-start.1 = (bf16[1024,128]{1,0:T(8,128)(2,1)S(1)}, bf16[1024,128]{1,0:T(8,128)(2,1)S(1)}, u32[]{:S(2)}, u32[]{:S(2)}) collective-permute-start(bf16[1024,128]{1,0:T(8,128)(2,1)S(1)} %collective-permute-done.refs_1_), channel_id=1, source_target_pairs={{0,16},{16,32},{32,48},{48,0},{64,80},{80,96},{96,112},{112,64},{1... | collective-permute-start | bytes 786440 | tf_op jit(solution)/shard_map/ppermute | solution.py:417
  53.0 20.5 %collective-permute-start.14 = (bf16[8192,128]{1,0:T(8,128)(2,1)}, bf16[8192,128]{1,0:T(8,128)(2,1)}, u32[]{:S(2)}, u32[]{:S(2)}) collective-permute-start(bf16[8192,128]{1,0:T(8,128)(2,1)} %get-tuple-element.20.refs_2_), channel_id=1, source_target_pairs={{0,1},{1,0},{2,3},{3,2},{4,5},{5,4},{6,7},{7,6},{8,9},{9,8},{10,11... | collective-permute-start | bytes 6291464 | tf_op jit(solution)/shard_map/ppermute | solution.py:421
  61.6 29.5 %collective-permute-start.16 = (bf16[2048,128]{1,0:T(8,128)(2,1)}, bf16[2048,128]{1,0:T(8,128)(2,1)S(1)}, u32[]{:S(2)}, u32[]{:S(2)}) collective-permute-start(bf16[2048,128]{1,0:T(8,128)(2,1)} %get-tuple-element.24), channel_id=1, source_target_pairs={{0,2},{1,3},{2,4},{3,5},{4,6},{5,7},{6,0},{7,1},{8,10},{9,11},{10,... | collective-permute-start | bytes 1572872 | tf_op jit(solution)/shard_map/ppermute | solution.py:412
  63.9 27.2 %collective-permute-start.17 = (bf16[2048,128]{1,0:T(8,128)(2,1)}, bf16[2048,128]{1,0:T(8,128)(2,1)S(1)}, u32[]{:S(2)}, u32[]{:S(2)}) collective-permute-start(bf16[2048,128]{1,0:T(8,128)(2,1)} %get-tuple-element.25), channel_id=1, source_target_pairs={{0,6},{1,7},{2,0},{3,1},{4,2},{5,3},{6,4},{7,5},{8,14},{9,15},{10,... | collective-permute-start | bytes 1572872 | tf_op jit(solution)/shard_map/ppermute | solution.py:412
  63.9 32.7 %collective-permute-start.18 = (bf16[2048,128]{1,0:T(8,128)(2,1)}, bf16[2048,128]{1,0:T(8,128)(2,1)S(1)}, u32[]{:S(2)}, u32[]{:S(2)}) collective-permute-start(bf16[2048,128]{1,0:T(8,128)(2,1)} %get-tuple-element.26), channel_id=1, source_target_pairs={{0,4},{1,5},{2,6},{3,7},{4,0},{5,1},{6,2},{7,3},{8,12},{9,13},{10,... | collective-permute-start | bytes 1572872 | tf_op jit(solution)/shard_map/ppermute | solution.py:412
  80.6 54.0 %all-to-all-start = ((bf16[8,512,128]{2,1,0:T(8,128)(2,1)}), bf16[8,512,128]{2,1,0:T(8,128)(2,1)S(1)}, u32[]{:S(2)}, u32[]{:S(2)}) async-start(bf16[8,512,128]{2,1,0:T(8,128)(2,1)} %bitcast.13), calls=%async_computation | async-start | bytes 2097152 | tf_op jit(solution)/shard_map/all_to_all | solution.py:425
  97.4 33.3 %collective-permute-start.19 = (bf16[1024,128]{1,0:T(8,128)(2,1)}, bf16[1024,128]{1,0:T(8,128)(2,1)S(1)}, u32[]{:S(2)}, u32[]{:S(2)}) collective-permute-start(bf16[1024,128]{1,0:T(8,128)(2,1)} %add_convert_fusion), channel_id=1, source_target_pairs={{0,8},{1,9},{2,10},{3,11},{4,12},{5,13},{6,14},{7,15},{8,0},{9,1},... | collective-permute-start | bytes 786440 | tf_op jit(solution)/shard_map/ppermute | solution.py:412
  107.1 20.3 %collective-permute-start.20 = (bf16[512,128]{1,0:T(8,128)(2,1)}, bf16[512,128]{1,0:T(8,128)(2,1)S(1)}, u32[]{:S(2)}, u32[]{:S(2)}) collective-permute-start(bf16[512,128]{1,0:T(8,128)(2,1)} %get-tuple-element.28), channel_id=1, source_target_pairs={{0,96},{16,112},{32,64},{48,80},{64,32},{80,48},{96,0},{112,16},{1... | collective-permute-start | bytes 393224 | tf_op jit(solution)/shard_map/ppermute | solution.py:417
  108.7 21.3 %collective-permute-start.21 = (bf16[512,128]{1,0:T(8,128)(2,1)}, bf16[512,128]{1,0:T(8,128)(2,1)S(1)}, u32[]{:S(2)}, u32[]{:S(2)}) collective-permute-start(bf16[512,128]{1,0:T(8,128)(2,1)} %get-tuple-element.29), channel_id=1, source_target_pairs={{0,80},{16,96},{32,112},{48,64},{64,16},{80,32},{96,48},{112,0},{1... | collective-permute-start | bytes 393224 | tf_op jit(solution)/shard_map/ppermute | solution.py:417
  114.4 24.5 %collective-permute-start.22 = (bf16[512,128]{1,0:T(8,128)(2,1)}, bf16[512,128]{1,0:T(8,128)(2,1)}, u32[]{:S(2)}, u32[]{:S(2)}) collective-permute-start(bf16[512,128]{1,0:T(8,128)(2,1)} %get-tuple-element.30), channel_id=1, source_target_pairs={{0,112},{16,64},{32,80},{48,96},{64,48},{80,0},{96,16},{112,32},{1... | collective-permute-start | bytes 393224 | tf_op jit(solution)/shard_map/ppermute | solution.py:417
  115.9 23.0 %collective-permute-start.23 = (bf16[512,128]{1,0:T(8,128)(2,1)}, bf16[512,128]{1,0:T(8,128)(2,1)}, u32[]{:S(2)}, u32[]{:S(2)}) collective-permute-start(bf16[512,128]{1,0:T(8,128)(2,1)} %get-tuple-element.31), channel_id=1, source_target_pairs={{0,64},{16,80},{32,96},{48,112},{64,0},{80,16},{96,32},{112,48},{1... | collective-permute-start | bytes 393224 | tf_op jit(solution)/shard_map/ppermute | solution.py:417
  127.3 11.5 %collective-permute-start.24 = (bf16[512,128]{1,0:T(8,128)(2,1)}, bf16[512,128]{1,0:T(8,128)(2,1)}, u32[]{:S(2)}, u32[]{:S(2)}) collective-permute-start(bf16[512,128]{1,0:T(8,128)(2,1)} %get-tuple-element.32), channel_id=1, source_target_pairs={{0,32},{16,48},{32,0},{48,16},{64,96},{80,112},{96,64},{112,80},{1... | collective-permute-start | bytes 393224 | tf_op jit(solution)/shard_map/ppermute | solution.py:417
  (17 other events, 132.4 us)
